TPU v7x, 256 devices: a whole 4x4x8 slice. The times are simulated.
256 devices in a mesh: gx: 4 (over z_lo), gy: 8 (over x, z_hi), gz: 8 (over y, core).
Axes of the slice: x: 4, y: 4, z: 8 (z_hi: 2, z_lo: 4; z = z_hi * 4 + z_lo), core: 2. Of those that a mesh axis runs over, the one named last changes fastest.
Arguments:
- attn_out: bfloat16 [16384, 8192], P('gx', ('gy', 'gz')), may hold values from -16 to 16
- out_grad: bfloat16 [16384, 8192], P('gx', ('gz', 'gy')), may hold values from -0.046875 to 0.046875
- valid_counts: int32 [16], P('gx'), may hold values from 128 to 1024
Outputs:
- weight_grad: float32 [8192, 8192], P(('gy', 'gx'), 'gz')
Inputs may be any that keep to these rules, and one draw needn't show every extreme that they name: `valid_counts`: valid tokens of a packed row come first, padding after.
All inputs are finite; a program needn't handle non-finite values.
Results may differ from a plain program's by a relative error of at most 0.0003.
Values may be sent and summed in bfloat16 or wider, within the bound.
A program may use at most 64 MiB of HBM per device.

v0:
```python
import jax
import jax.numpy as jnp
from jax import lax
from jax.sharding import Mesh
from jax.sharding import PartitionSpec as P

GY = ("gy_0", "gy_1")
GY_GZ = ("gy_0", "gy_1", "gz")
GZ_GY = ("gz", "gy_0", "gy_1")
GY_GX = ("gy_0", "gy_1", "gx")


def whole_of(value, axes, dim):
    out = value
    for number in range(len(axes) - 1, -1, -1):
        out = lax.all_gather(out, axes[number], axis=dim, tiled=True)
    return out


def split_up(value, dim, peers):
    lengths = value.shape
    tiles = value.reshape(*lengths[:dim], peers, lengths[dim] // peers, *lengths[dim + 1 :])
    return jnp.moveaxis(tiles, dim, 0)


def summed_on_arrival(value, axis, dim):
    tiles = split_up(value, dim, lax.axis_size(axis))
    arrived = lax.all_to_all(tiles, axis, split_axis=0, concat_axis=0, tiled=True)
    return arrived.sum(axis=0)


def transpose_product(inputs, grads):
    return lax.dot_general(
        inputs, grads, (((0,), (0,)), ((), ())), preferred_element_type=jnp.float32
    )


def shards(attn_out, out_grad, valid_counts):
    rows_here = valid_counts.shape[0]
    slot_count = attn_out.shape[0] // rows_here
    positions = lax.broadcasted_iota(jnp.int32, (rows_here, slot_count), 1)
    kept_rows = (positions < valid_counts[:, None]).reshape(-1)
    gathered_inputs = lax.all_gather(attn_out, "gz", axis=1, tiled=True)
    gathered_grads = whole_of(out_grad, GY, 1)
    masked = jnp.where(kept_rows[:, None], gathered_grads, jnp.zeros((), gathered_grads.dtype))
    partial_grad = transpose_product(gathered_inputs, masked)
    return summed_on_arrival(partial_grad, "gx", 0)


def solution(mesh):
    split = Mesh(
        mesh.devices.reshape(mesh.shape["gx"], 4, 2, mesh.shape["gz"]), ("gx", "gy_0", "gy_1", "gz")
    )
    return jax.shard_map(
        shards,
        mesh=split,
        in_specs=(P("gx", GY_GZ), P("gx", GZ_GY), P("gx")),
        out_specs=P(GY_GX, "gz"),
        check_vma=False,
    )
```

profile of v0, /device:TPU:8, one launch (start us, length us, event | category | flops | bytes accessed | tf_op | source)
XLA Modules:
  0.0 345.3 jit_solution(17290514149555261762)
XLA Ops:
  6.5 0.0 all-gather.4.cloned.1.call-start
  6.5 0.7 all-gather.4.cloned.1.call-update
  7.3 0.0 all-gather.8.cloned.1.call-start
  7.3 0.7 all-gather.8.cloned.1.call-update
  8.0 0.0 all-gather.6.cloned.1.call-start
  8.1 69.1 %all-gather.4.cloned.1.call-done = bf16[4096,256]{1,0:T(8,128)(2,1)} async-done(((bf16[4096,128]{1,0:T(8,128)(2,1)}), bf16[4096,256]{1,0:T(8,128)(2,1)}) %all-gather.4.cloned.1.call-update) | async-done | bytes 2097168 | tf_op jit(solution)/shard_map/all_gather | solution.py:16
  77.1 0.0 all-gather.6.cloned.1.call-update
  77.2 0.7 fusion.4
  77.9 53.2 %all-gather.8.cloned.1.call-done = bf16[4096,1024]{1,0:T(8,128)(2,1)} async-done(((bf16[4096,128]{1,0:T(8,128)(2,1)}), bf16[4096,1024]{1,0:T(8,128)(2,1)}) %all-gather.8.cloned.1.call-update) | async-done | bytes 8388624 | tf_op jit(solution)/shard_map/all_gather | solution.py:43
  131.1 92.2 %all-gather.6.cloned.1.call-done = bf16[4096,1024]{1,0:T(8,128)(2,1)} async-done(((bf16[4096,256]{1,0:T(8,128)(2,1)}), bf16[4096,1024]{1,0:T(8,128)(2,1)}) %all-gather.6.cloned.1.call-update) | async-done | bytes 8388624 | tf_op jit(solution)/shard_map/all_gather | solution.py:16
  223.3 15.3 %fusion = f32[1024,1024]{0,1:T(8,128)S(1)} fusion(bf16[4096,1024]{1,0:T(8,128)(2,1)} %all-gather.8.cloned.1.call-done, bf16[4096,1024]{1,0:T(8,128)(2,1)} %all-gather.6.cloned.1.call-done, pred[4096]{0:T(1024)(128)(4,1)S(1)} %bitcast.10), kind=kOutput, calls=%fused_computation | convolution fusion | flops 8594128896 | bytes 20975616 | tf_op jit(solution)/shard_map/dot_general | solution.py:33
  238.6 96.5 %all_to_all.5 = f32[4,256,1024]{2,1,0:T(8,128)} all-to-all(f32[4,256,1024]{2,1,0:T(8,128)S(1)} %bitcast.9), channel_id=1, replica_groups=mesh['gx'=4,'gy_0'=4,'gy_1'=2,'gz'=8] {'gx'}, dimensions={0} | all-to-all | bytes 8388608 | tf_op jit(solution)/shard_map/all_to_all | solution.py:28
  335.1 3.7 %reduce_sum.9 = f32[256,1024]{1,0:T(8,128)} reduce(f32[4,256,1024]{2,1,0:T(8,128)} %all_to_all.5, f32[]{:T(128)} %constant.1.clone.1), dimensions={0}, to_apply=%region_0.1 | reduce | flops 786432 | bytes 5242884 | tf_op jit(solution)/shard_map/reduce_sum | solution.py:29
  (1 shorter events, 0.0 us)
Async XLA Ops:
  6.5 70.6 %all-gather.4.cloned.1.call-start = ((), (), s32[]{:S(2)}) async-start(), calls=%async_computation.1 | async-start | bytes 3145728 | tf_op jit(solution)/shard_map/all_gather | solution.py:16
  7.3 123.8 %all-gather.8.cloned.1.call-start = ((), (), s32[]{:S(2)}) async-start(), calls=%async_computation.3 | async-start | bytes 9437184 | tf_op jit(solution)/shard_map/all_gather | solution.py:43
  8.0 215.3 %all-gather.6.cloned.1.call-start = ((), (), s32[]{:S(2)}) async-start(), calls=%async_computation.2 | async-start | bytes 10485760 | tf_op jit(solution)/shard_map/all_gather | solution.py:16
Sparse Core Ops, SparseCore 0:
  9.1 67.9 all-gather.3
  79.0 52.0 all-gather.7
  132.9 90.3 all-gather.5
where the time goes:
time: 345 us
  waiting for transfers between devices  216 us (63%)
  blocking collectives  96.5 us (28%)
  matrix products  15.3 us (4%)
  between operations  13.1 us (4%)
  other arithmetic  4.42 us (1%)
    all_gather x2, waiting for transfers between devices, whole_of(): out = lax.all_gather(out, axes[number], axis=dim, tiled=True)  161 us
    all_to_all x1, blocking collectives, summed_on_arrival(): lax.all_to_all(tiles, axis, split_axis=0, concat_axis=0, tiled=True)  96.5 us
    all_gather x1, waiting for transfers between devices, shards(): gathered_inputs = lax.all_gather(attn_out, 'gz', axis=1, tiled=True)  53.2 us
    dot_general x1, matrix products, transpose_product(): lax.dot_general(inputs, grads, (((0,), (0,)), ((), ())), preferred_elemen...  15.3 us
  transfers between devices with their start and end apart: 3, of which 3 were waited for; matrix products, arithmetic and copies ran while one was open for 0% of the time, Pallas kernels for 0%

commit v1 on v0

--- a/solution.py
+++ b/solution.py
@@ -40,7 +40,29 @@
     slot_count = attn_out.shape[0] // rows_here
     positions = lax.broadcasted_iota(jnp.int32, (rows_here, slot_count), 1)
     kept_rows = (positions < valid_counts[:, None]).reshape(-1)
-    gathered_inputs = lax.all_gather(attn_out, "gz", axis=1, tiled=True)
+    finding = lax.axis_size("gz")
+    e_now = lax.axis_index("gz")
+    later, back, arr_out = (finding, e_now, attn_out.shape[1])
+    shelf = [(ii, (ii + 1) % later) for ii in range(later)]
+    blocks_here = [(ii, (ii - 1) % later) for ii in range(later)]
+    gathered_inputs = jnp.zeros(
+        (*attn_out.shape[:1], later * arr_out, *attn_out.shape[2:]), attn_out.dtype
+    )
+    gathered_inputs = lax.dynamic_update_slice_in_dim(
+        gathered_inputs, attn_out, back * arr_out, axis=1
+    )
+    response = block_out = attn_out
+    x_next = later // 2
+    for q in tuple(range(1, x_next + 1)):
+        response = lax.ppermute(response, "gz", shelf)
+        gathered_inputs = lax.dynamic_update_slice_in_dim(
+            gathered_inputs, response, (back - q) % later * arr_out, axis=1
+        )
+        if q < later - x_next:
+            block_out = lax.ppermute(block_out, axis_name="gz", perm=blocks_here)
+            gathered_inputs = lax.dynamic_update_slice_in_dim(
+                gathered_inputs, block_out, (back + q) % later * arr_out, axis=1
+            )
     gathered_grads = whole_of(out_grad, GY, 1)
     masked = jnp.where(kept_rows[:, None], gathered_grads, jnp.zeros((), gathered_grads.dtype))
     partial_grad = transpose_product(gathered_inputs, masked)

time: 345 us -> 286 us (0.83)
  waiting for transfers between devices: 216 us -> 137 us
  local copies, waits for them, and re-layouts: 0.01 us -> 14.6 us
  starting transfers between devices: 0.08 us -> 5.92 us
    all_gather x2, waiting for transfers between devices: 161 us -> 98.6 us  [whole_of(): out = lax.all_gather(out, axes[number], axis=dim, tiled=True)]
    all_gather x1 -> x0, waiting for transfers between devices: 53.2 us -> none  [shards(): gathered_inputs = lax.all_gather(attn_out, 'gz', axis=1, tiled=True)]
    ppermute x0 -> x7, waiting for transfers between devices: none -> 37.9 us  [the longest x4 33 us: shards(): response = lax.ppermute(response, 'gz', shelf)]
    dynamic_update_slice x0 -> x8, local copies, waits for them, and re-layouts: none -> 10.3 us  [the longest x4 5.83 us: shards(): lax.dynamic_update_slice_in_dim(gathered_inputs, response, (back - q) % l...]
    ppermute x0 -> x7, starting transfers between devices: none -> 5.88 us  [the longest x3 5.86 us: shards(): block_out = lax.ppermute(block_out, axis_name='gz', perm=blocks_here)]
    broadcast_in_dim x0 -> x1, local copies, waits for them, and re-layouts: none -> 4.31 us  [shards(): jnp.zeros((*attn_out.shape[:1], later * arr_out, *attn_out.shape[2:]), at...]
  transfers between devices with their start and end apart: 3 -> 9, of which waited for: 3 -> 8; matrix products, arithmetic and copies ran while one was open for 0% -> 5% of each run, Pallas kernels for 0% -> 0%
where the time goes in v1:
time: 286 us
  waiting for transfers between devices  137 us (48%)
  blocking collectives  96.5 us (34%)
  matrix products  14.8 us (5%)
  local copies, waits for them, and re-layouts  14.6 us (5%)
  between operations  13.5 us (5%)
  starting transfers between devices  5.92 us (2%)
  other arithmetic  3.76 us (1%)
    all_gather x2, waiting for transfers between devices, whole_of(): out = lax.all_gather(out, axes[number], axis=dim, tiled=True)  98.6 us
    all_to_all x1, blocking collectives, summed_on_arrival(): lax.all_to_all(tiles, axis, split_axis=0, concat_axis=0, tiled=True)  96.5 us
    ppermute x4, waiting for transfers between devices, shards(): response = lax.ppermute(response, 'gz', shelf)  33 us
    dot_general x1, matrix products, transpose_product(): lax.dot_general(inputs, grads, (((0,), (0,)), ((), ())), preferred_elemen...  14.8 us
    ppermute x3, starting transfers between devices, shards(): block_out = lax.ppermute(block_out, axis_name='gz', perm=blocks_here)  5.86 us
    dynamic_update_slice x4, local copies, waits for them, and re-layouts, shards(): lax.dynamic_update_slice_in_dim(gathered_inputs, response, (back - q) % l...  5.83 us
  transfers between devices with their start and end apart: 9, of which 8 were waited for; matrix products, arithmetic and copies ran while one was open for 5% of the time, Pallas kernels for 0%

profile of v1, /device:TPU:8, one launch (start us, length us, event | category | flops | bytes accessed | tf_op | source)
XLA Modules:
  0.0 286.3 jit_solution(7970154354244863458)
XLA Ops:
  6.5 0.0 copy-start
  6.5 0.0 copy-start.1
  6.5 0.0 all-gather.3.cloned.1.call-start
  6.5 0.7 all-gather.3.cloned.1.call-update
  7.3 0.0 all-gather.5.cloned.1.call-start
  7.3 69.8 %all-gather.3.cloned.1.call-done = bf16[4096,256]{1,0:T(8,128)(2,1)} async-done(((bf16[4096,128]{1,0:T(8,128)(2,1)}), bf16[4096,256]{1,0:T(8,128)(2,1)}) %all-gather.3.cloned.1.call-update) | async-done | bytes 2097168 | tf_op jit(solution)/shard_map/all_gather | solution.py:16
  77.2 0.0 all-gather.5.cloned.1.call-update
  77.2 0.0 collective-permute-start
  77.2 1.7 collective-permute-start.1
  78.9 12.8 %collective-permute-done = bf16[4096,128]{1,0:T(8,128)(2,1)} collective-permute-done((bf16[4096,128]{1,0:T(8,128)(2,1)}, bf16[4096,128]{1,0:T(8,128)(2,1)}, u32[]{:S(2)}, u32[]{:S(2)}) %collective-permute-start) | collective-permute-done | bytes 1048608 | tf_op jit(solution)/shard_map/ppermute | solution.py:57
  91.7 0.0 collective-permute-start.2
  91.7 4.3 %broadcast_in_dim.14 = bf16[4096,1024]{1,0:T(8,128)(2,1)} broadcast(bf16[]{:T(256)} %constant.51.clone.1), dimensions={} | broadcast | bytes 8388610 | tf_op jit(solution)/shard_map/broadcast_in_dim | solution.py:48
  96.0 0.0 copy-done
  96.0 1.1 constant_dynamic-update-slice_fusion.7
  97.1 0.0 collective-permute-done.1
  97.1 1.8 collective-permute-start.3
  99.0 0.0 copy-done.1
  99.0 0.1 fusion.4
  99.1 7.0 %collective-permute-done.2 = bf16[4096,128]{1,0:T(8,128)(2,1)S(1)} collective-permute-done((bf16[4096,128]{1,0:T(8,128)(2,1)}, bf16[4096,128]{1,0:T(8,128)(2,1)S(1)}, u32[]{:S(2)}, u32[]{:S(2)}) %collective-permute-start.2) | collective-permute-done | bytes 1048608 | tf_op jit(solution)/shard_map/ppermute | solution.py:57
  106.2 0.0 collective-permute-start.4
  106.2 2.4 constant_dynamic-update-slice_fusion.6
  108.6 1.1 constant_dynamic-update-slice_fusion.5
  109.7 1.6 collective-permute-done.3
  111.3 2.3 collective-permute-start.5
  113.6 1.2 constant_dynamic-update-slice_fusion.4
  114.8 5.6 %collective-permute-done.4 = bf16[4096,128]{1,0:T(8,128)(2,1)S(1)} collective-permute-done((bf16[4096,128]{1,0:T(8,128)(2,1)S(1)}, bf16[4096,128]{1,0:T(8,128)(2,1)S(1)}, u32[]{:S(2)}, u32[]{:S(2)}) %collective-permute-start.4) | collective-permute-done | bytes 1048608 | tf_op jit(solution)/shard_map/ppermute | solution.py:57
  120.4 0.0 collective-permute-start.6
  120.4 1.1 constant_dynamic-update-slice_fusion.3
  121.5 1.1 constant_dynamic-update-slice_fusion.2
  122.6 3.3 %collective-permute-done.5 = bf16[4096,128]{1,0:T(8,128)(2,1)S(1)} collective-permute-done((bf16[4096,128]{1,0:T(8,128)(2,1)S(1)}, bf16[4096,128]{1,0:T(8,128)(2,1)S(1)}, u32[]{:S(2)}, u32[]{:S(2)}) %collective-permute-start.5) | collective-permute-done | bytes 1048608 | tf_op jit(solution)/shard_map/ppermute | solution.py:62
  125.9 1.1 constant_dynamic-update-slice_fusion.1
  127.0 7.6 %collective-permute-done.6 = bf16[4096,128]{1,0:T(8,128)(2,1)S(1)} collective-permute-done((bf16[4096,128]{1,0:T(8,128)(2,1)S(1)}, bf16[4096,128]{1,0:T(8,128)(2,1)S(1)}, u32[]{:S(2)}, u32[]{:S(2)}) %collective-permute-start.6) | collective-permute-done | bytes 1048608 | tf_op jit(solution)/shard_map/ppermute | solution.py:57
  134.6 1.1 constant_dynamic-update-slice_fusion
  135.7 28.7 %all-gather.5.cloned.1.call-done = bf16[4096,1024]{1,0:T(8,128)(2,1)} async-done(((bf16[4096,256]{1,0:T(8,128)(2,1)}), bf16[4096,1024]{1,0:T(8,128)(2,1)}) %all-gather.5.cloned.1.call-update) | async-done | bytes 8388624 | tf_op jit(solution)/shard_map/all_gather | solution.py:16
  164.5 14.8 %fusion = f32[1024,1024]{1,0:T(8,128)S(1)} fusion(bf16[4096,1024]{1,0:T(8,128)(2,1)} %constant_dynamic-update-slice_fusion, bf16[4096,1024]{1,0:T(8,128)(2,1)} %all-gather.5.cloned.1.call-done, pred[4096]{0:T(1024)(128)(4,1)S(1)} %bitcast.8), kind=kOutput, calls=%fused_computation | convolution fusion | flops 8594128896 | bytes 20975616 | tf_op jit(solution)/shard_map/dot_general | solution.py:33
  179.3 96.5 %all_to_all.5 = f32[4,256,1024]{2,1,0:T(8,128)} all-to-all(f32[4,256,1024]{2,1,0:T(8,128)S(1)} %bitcast.7), channel_id=1, replica_groups=mesh['gx'=4,'gy_0'=4,'gy_1'=2,'gz'=8] {'gx'}, dimensions={0} | all-to-all | bytes 8388608 | tf_op jit(solution)/shard_map/all_to_all | solution.py:28
  275.8 3.7 %reduce_sum.9 = f32[256,1024]{1,0:T(8,128)} reduce(f32[4,256,1024]{2,1,0:T(8,128)} %all_to_all.5, f32[]{:T(128)} %constant.65.clone.1), dimensions={0}, to_apply=%region_0.1 | reduce | flops 786432 | bytes 5242884 | tf_op jit(solution)/shard_map/reduce_sum | solution.py:29
  (1 shorter events, 0.0 us)
Async XLA Ops:
  6.5 89.5 %copy-start = (bf16[4096,128]{1,0:T(8,128)(2,1)S(1)}, bf16[4096,128]{1,0:T(8,128)(2,1)}, u32[]{:S(2)}) copy-start(bf16[4096,128]{1,0:T(8,128)(2,1)} %param.3) | copy-start | bytes 3145732
  6.5 92.4 %copy-start.1 = (s32[4]{0:T(128)S(1)}, s32[4]{0:T(128)}, u32[]{:S(2)}) copy-start(s32[4]{0:T(128)} %param.5) | copy-start | bytes 52
  6.5 70.6 %all-gather.3.cloned.1.call-start = ((), (), s32[]{:S(2)}) async-start(), calls=%async_computation.1 | async-start | bytes 3145728 | tf_op jit(solution)/shard_map/all_gather | solution.py:16
  7.3 157.2 %all-gather.5.cloned.1.call-start = ((), (), s32[]{:S(2)}) async-start(), calls=%async_computation.2 | async-start | bytes 10485760 | tf_op jit(solution)/shard_map/all_gather | solution.py:16
  77.2 14.6 %collective-permute-start = (bf16[4096,128]{1,0:T(8,128)(2,1)}, bf16[4096,128]{1,0:T(8,128)(2,1)}, u32[]{:S(2)}, u32[]{:S(2)}) collective-permute-start(bf16[4096,128]{1,0:T(8,128)(2,1)} %param.3), channel_id=1, source_target_pairs={{0,1},{1,2},{2,3},{3,4},{4,5},{5,6},{6,7},{7,0},{8,9},{9,10},{10,1... | collective-permute-start | bytes 3145736 | tf_op jit(solution)/shard_map/ppermute | solution.py:57
  77.2 19.9 %collective-permute-start.1 = (bf16[4096,128]{1,0:T(8,128)(2,1)}, bf16[4096,128]{1,0:T(8,128)(2,1)S(1)}, u32[]{:S(2)}, u32[]{:S(2)}) collective-permute-start(bf16[4096,128]{1,0:T(8,128)(2,1)} %param.3), channel_id=1, source_target_pairs={{0,7},{1,0},{2,1},{3,2},{4,3},{5,4},{6,5},{7,6},{8,15},{9,8},{10,9... | collective-permute-start | bytes 3145736 | tf_op jit(solution)/shard_map/ppermute | solution.py:62
  91.7 14.4 %collective-permute-start.2 = (bf16[4096,128]{1,0:T(8,128)(2,1)}, bf16[4096,128]{1,0:T(8,128)(2,1)S(1)}, u32[]{:S(2)}, u32[]{:S(2)}) collective-permute-start(bf16[4096,128]{1,0:T(8,128)(2,1)} %collective-permute-done), channel_id=1, source_target_pairs={{0,1},{1,2},{2,3},{3,4},{4,5},{5,6},{6,7},{7,0},{8,9},{9,10},{10,1... | collective-permute-start | bytes 3145736 | tf_op jit(solution)/shard_map/ppermute | solution.py:57
  97.1 14.1 %collective-permute-start.3 = (bf16[4096,128]{1,0:T(8,128)(2,1)S(1)}, bf16[4096,128]{1,0:T(8,128)(2,1)S(1)}, u32[]{:S(2)}, u32[]{:S(2)}) collective-permute-start(bf16[4096,128]{1,0:T(8,128)(2,1)S(1)} %collective-permute-done.1), channel_id=1, source_target_pairs={{0,7},{1,0},{2,1},{3,2},{4,3},{5,4},{6,5},{7,6},{8,15},{9,8},{10,9... | collective-permute-start | bytes 3145736 | tf_op jit(solution)/shard_map/ppermute | solution.py:62
  106.2 14.2 %collective-permute-start.4 = (bf16[4096,128]{1,0:T(8,128)(2,1)S(1)}, bf16[4096,128]{1,0:T(8,128)(2,1)S(1)}, u32[]{:S(2)}, u32[]{:S(2)}) collective-permute-start(bf16[4096,128]{1,0:T(8,128)(2,1)S(1)} %collective-permute-done.2), channel_id=1, source_target_pairs={{0,1},{1,2},{2,3},{3,4},{4,5},{5,6},{6,7},{7,0},{8,9},{9,10},{10,1... | collective-permute-start | bytes 3145736 | tf_op jit(solution)/shard_map/ppermute | solution.py:57
  111.3 14.6 %collective-permute-start.5 = (bf16[4096,128]{1,0:T(8,128)(2,1)S(1)}, bf16[4096,128]{1,0:T(8,128)(2,1)S(1)}, u32[]{:S(2)}, u32[]{:S(2)}) collective-permute-start(bf16[4096,128]{1,0:T(8,128)(2,1)S(1)} %collective-permute-done.3), channel_id=1, source_target_pairs={{0,7},{1,0},{2,1},{3,2},{4,3},{5,4},{6,5},{7,6},{8,15},{9,8},{10,9... | collective-permute-start | bytes 3145736 | tf_op jit(solution)/shard_map/ppermute | solution.py:62
  120.4 14.2 %collective-permute-start.6 = (bf16[4096,128]{1,0:T(8,128)(2,1)S(1)}, bf16[4096,128]{1,0:T(8,128)(2,1)S(1)}, u32[]{:S(2)}, u32[]{:S(2)}) collective-permute-start(bf16[4096,128]{1,0:T(8,128)(2,1)S(1)} %collective-permute-done.4), channel_id=1, source_target_pairs={{0,1},{1,2},{2,3},{3,4},{4,5},{5,6},{6,7},{7,0},{8,9},{9,10},{10,1... | collective-permute-start | bytes 3145736 | tf_op jit(solution)/shard_map/ppermute | solution.py:57
Sparse Core Ops, SparseCore 0:
  9.1 67.9 all-gather.2
  79.0 85.4 all-gather.4
